TPU v7x, 32 devices: a whole 2x2x4 slice. The times are simulated.
32 devices in a mesh: dp: 8 (over y, x, core), tensor: 4 (over z).
Axes of the slice: x: 2, y: 2, z: 4, core: 2. Of those that a mesh axis runs over, the one named last changes fastest.
Arguments:
- inputs: bfloat16 [12288, 768], P(('dp', 'tensor')), may hold values from -6 to 6
- segments: int32 [24, 512], P('dp'), may hold values from 0 to 3, never falling along the last dimension, each value on 1 to 256 neighbouring positions
- labels: int32 [24], P('dp'), may hold values from 0 to 2
- qkv_weight: bfloat16 [3, 768, 768], P(None, None, 'tensor'), may hold values from -0.21875 to 0.21875
- qv_bias: float32 [2, 768], P(None, 'tensor'), may hold values from -3 to 3
- out_weight: bfloat16 [768, 768], P('tensor'), may hold values from -0.875 to 0.875
- out_bias: float32 [768], replicated, may hold values from -3 to 3
- norm1_gain: float32 [768], replicated, may hold values from 0.5 to 1.5
- norm1_bias: float32 [768], replicated, may hold values from -3 to 3
- up_weight: bfloat16 [768, 3072], P(None, 'tensor'), may hold values from -0.21875 to 0.21875
- up_bias: float32 [3072], P('tensor'), may hold values from -3 to 3
- down_weight: bfloat16 [3072, 768], P('tensor'), may hold values from -0.109375 to 0.109375
- down_bias: float32 [768], replicated, may hold values from -3 to 3
- norm2_gain: float32 [768], replicated, may hold values from 0.5 to 1.5
- norm2_bias: float32 [768], replicated, may hold values from -3 to 3
- pool_weight: bfloat16 [768, 768], replicated, may hold values from -0.21875 to 0.21875
- pool_bias: float32 [768], replicated, may hold values from -3 to 3
- class_weight: bfloat16 [768, 3], replicated, may hold values from -0.4375 to 0.4375
- class_bias: float32 [3], replicated, may hold values from -4 to 4
- cotangent: bfloat16 [12288, 768], P(('dp', 'tensor')), may hold values from -6 to 6
Outputs:
- hidden: bfloat16 [12288, 768], P(('dp', 'tensor'))
- input_grad: bfloat16 [12288, 768], P(('dp', 'tensor'))
- qkv_weight_grad: float32 [3, 768, 768], P(None, 'dp', 'tensor')
- qv_bias_grad: float32 [2, 768], P(None, 'tensor')
- out_weight_grad: float32 [768, 768], P('tensor', 'dp')
- out_bias_grad: float32 [768], replicated
- norm1_gain_grad: float32 [768], replicated
- norm1_bias_grad: float32 [768], replicated
- up_weight_grad: float32 [768, 3072], P('dp', 'tensor')
- up_bias_grad: float32 [3072], P('tensor')
- down_weight_grad: float32 [3072, 768], P('tensor', 'dp')
- down_bias_grad: float32 [768], replicated
- norm2_gain_grad: float32 [768], replicated
- norm2_bias_grad: float32 [768], replicated
- pool_weight_grad: float32 [768, 768], replicated
- pool_bias_grad: float32 [768], replicated
- class_weight_grad: float32 [768, 3], replicated
- class_bias_grad: float32 [3], replicated
Inputs may be any that keep to these rules, and one draw needn't show every extreme that they name: `segments`: along each packed row of 512 tokens the ids never fall; a document holds at most half of 512 tokens.
All inputs are finite; a program needn't handle non-finite values.
Results may differ from a plain program's by a relative error of at most 0.017.
The roundings to bfloat16 on the way count: a program that leaves them out, or rounds other values in their place, can miss the bound.
Values may be sent and summed in bfloat16 or wider, within the bound.
A program may use at most 128 MiB of HBM per device.

v0:
```python
from functools import partial
import jax
import jax.numpy as jnp
from jax import lax
from jax.sharding import PartitionSpec as P

HEAD = 64
epsilon = 1e-12
masked_value = -1e30


def norm_forward(values, norm_gain, norm_shift):
    centre = values - jnp.mean(values, axis=-1, keepdims=True)
    inverse = lax.rsqrt(jnp.mean(centre * centre, axis=-1, keepdims=True) + epsilon)
    normed = centre * inverse
    return (normed * norm_gain + norm_shift, normed, inverse)


def norm_backward(grad_out, normed, inverse, norm_gain):
    scaled = grad_out * norm_gain
    grad_in = inverse * (
        scaled
        - jnp.mean(scaled, axis=-1, keepdims=True)
        - normed * jnp.mean(scaled * normed, axis=-1, keepdims=True)
    )
    return (grad_in, jnp.sum(grad_out * normed, axis=0), jnp.sum(grad_out, axis=0))


def split_heads(rows):
    return rows.reshape(rows.shape[0], rows.shape[1] // HEAD, HEAD)


def masked_scores(query_heads, key_heads, segment_row):
    raw_scores = jnp.einsum(
        "qhe,khe->hqk", query_heads, key_heads, preferred_element_type=jnp.float32
    ) * HEAD ** (-0.5)
    allowed = segment_row[:, None] == segment_row[None, :]
    return (jnp.where(allowed[None], raw_scores, masked_value), allowed)


def attend_sequence(block_items):
    query_seq, key_seq, value_seq, segment_row = block_items
    scores, allowed = masked_scores(split_heads(query_seq), split_heads(key_seq), segment_row)
    largest = jnp.max(scores, axis=-1, keepdims=True)
    exponent = jnp.exp(scores - largest)
    row_total = jnp.sum(exponent, axis=-1, keepdims=True)
    soft_low = (exponent / row_total).astype(jnp.bfloat16)
    context = jnp.einsum(
        "hqk,khe->qhe", soft_low, split_heads(value_seq), preferred_element_type=jnp.float32
    )
    context = context.reshape(query_seq.shape).astype(jnp.bfloat16)
    return (context, largest[..., 0] + jnp.log(row_total[..., 0]))


def attend_backward(block_items):
    query_seq, key_seq, value_seq, segment_row, log_total, grad_context = block_items
    query_heads = split_heads(query_seq)
    key_heads = split_heads(key_seq)
    value_heads = split_heads(value_seq)
    grad_heads = split_heads(grad_context)
    scores, allowed = masked_scores(query_heads, key_heads, segment_row)
    soft_probs = jnp.exp(scores - log_total[..., None])
    grad_values = jnp.einsum(
        "hqk,qhe->khe",
        soft_probs.astype(jnp.bfloat16),
        grad_heads,
        preferred_element_type=jnp.float32,
    )
    grad_soft = jnp.einsum(
        "qhe,khe->hqk", grad_heads, value_heads, preferred_element_type=jnp.float32
    )
    grad_scores = soft_probs * (grad_soft - jnp.sum(soft_probs * grad_soft, axis=-1, keepdims=True))
    grad_low = jnp.where(allowed[None], grad_scores, 0.0).astype(jnp.bfloat16)
    score_scale = HEAD ** (-0.5)
    grad_queries = (
        jnp.einsum("hqk,khe->qhe", grad_low, key_heads, preferred_element_type=jnp.float32)
        * score_scale
    )
    grad_keys = (
        jnp.einsum("hqk,qhe->khe", grad_low, query_heads, preferred_element_type=jnp.float32)
        * score_scale
    )
    full_shape = query_seq.shape
    return (
        grad_queries.reshape(full_shape).astype(jnp.bfloat16),
        grad_keys.reshape(full_shape).astype(jnp.bfloat16),
        grad_values.reshape(full_shape).astype(jnp.bfloat16),
    )


def body(
    inputs,
    segments,
    labels,
    qkv_weight,
    qv_bias,
    out_weight,
    out_bias,
    norm1_gain,
    norm1_bias,
    up_weight,
    up_bias,
    down_weight,
    down_bias,
    norm2_gain,
    norm2_bias,
    pool_weight,
    pool_bias,
    class_weight,
    class_bias,
    cotangent,
):
    share_rows = inputs.shape[0]
    seq_count, seq_length = segments.shape
    offset = lax.axis_index("tensor") * share_rows

    def take_share(array):
        return lax.dynamic_slice_in_dim(array, offset, share_rows, 0)

    gathered = lax.all_gather(inputs, "tensor", axis=0, tiled=True)
    group_rows = gathered.shape[0]
    projected = jnp.einsum("td,kde->kte", gathered, qkv_weight, preferred_element_type=jnp.float32)
    queries = (projected[0] + qv_bias[0]).astype(jnp.bfloat16)
    key_rows = projected[1].astype(jnp.bfloat16)
    value_rows = (projected[2] + qv_bias[1]).astype(jnp.bfloat16)
    local_width = queries.shape[1]

    def by_sequence(rows):
        return rows.reshape(seq_count, seq_length, rows.shape[-1])

    context, log_totals = lax.map(
        attend_sequence,
        (by_sequence(queries), by_sequence(key_rows), by_sequence(value_rows), segments),
    )
    context = context.reshape(group_rows, local_width)
    attended_all = (
        lax.psum(jnp.dot(context, out_weight, preferred_element_type=jnp.float32), "tensor")
        + out_bias
    )
    first_whole, normed_whole, inverse_whole = norm_forward(
        gathered.astype(jnp.float32) + attended_all, norm1_gain, norm1_bias
    )
    first_all = first_whole.astype(jnp.bfloat16)
    normed_one = take_share(normed_whole)
    inverse_one = take_share(inverse_whole)
    up_pre = jnp.dot(first_all, up_weight, preferred_element_type=jnp.float32) + up_bias
    gelu_exact = partial(jax.nn.gelu, approximate=False)
    active = gelu_exact(up_pre).astype(jnp.bfloat16)
    ffn_all = (
        lax.psum(jnp.dot(active, down_weight, preferred_element_type=jnp.float32), "tensor")
        + down_bias
    )
    final_whole, normed_all, inverse_all = norm_forward(
        first_whole + ffn_all, norm2_gain, norm2_bias
    )
    final_norm = take_share(final_whole)
    normed_two = take_share(normed_all)
    inverse_two = take_share(inverse_all)
    positions = offset + jnp.arange(share_rows, dtype=jnp.int32)
    row_starts = jnp.arange(seq_count, dtype=jnp.int32) * seq_length
    selector = (row_starts[:, None] == positions[None, :]).astype(jnp.float32)
    leading_part = jnp.dot(selector, final_norm, precision=lax.Precision.HIGHEST)
    leading = lax.psum(leading_part, "tensor").astype(jnp.bfloat16)
    pooled = jnp.tanh(jnp.dot(leading, pool_weight, preferred_element_type=jnp.float32) + pool_bias)
    pooled_low = pooled.astype(jnp.bfloat16)
    logits = jnp.dot(pooled_low, class_weight, preferred_element_type=jnp.float32) + class_bias
    chosen = (
        labels[:, None] == jnp.arange(class_weight.shape[1], dtype=jnp.int32)[None, :]
    ).astype(jnp.float32)
    grad_logits = (jax.nn.softmax(logits, axis=-1) - chosen).astype(jnp.bfloat16)
    class_weight_grad = jnp.einsum(
        "rd,rc->dc", pooled_low, grad_logits, preferred_element_type=jnp.float32
    )
    class_bias_grad = jnp.sum(grad_logits.astype(jnp.float32), axis=0)
    grad_pre = (
        jnp.einsum("rc,dc->rd", grad_logits, class_weight, preferred_element_type=jnp.float32)
        * (1.0 - pooled * pooled)
    ).astype(jnp.bfloat16)
    pool_weight_grad = jnp.einsum(
        "rd,re->de", leading, grad_pre, preferred_element_type=jnp.float32
    )
    pool_bias_grad = jnp.sum(grad_pre.astype(jnp.float32), axis=0)
    grad_leading = jnp.einsum(
        "re,de->rd", grad_pre, pool_weight, preferred_element_type=jnp.float32
    )
    grad_final = cotangent.astype(jnp.float32) + jnp.einsum(
        "rt,rd->td", selector, grad_leading, precision=lax.Precision.HIGHEST
    )
    grad_second, norm2_gain_grad, norm2_bias_grad = norm_backward(
        grad_final, normed_two, inverse_two, norm2_gain
    )
    grad_fed = grad_second.astype(jnp.bfloat16)
    down_bias_grad = jnp.sum(grad_fed.astype(jnp.float32), axis=0)
    grad_fed_all = lax.all_gather(grad_fed, "tensor", axis=0, tiled=True)
    down_weight_grad = jnp.einsum(
        "tf,td->fd", active, grad_fed_all, preferred_element_type=jnp.float32
    )
    grad_active = jnp.einsum(
        "td,fd->tf", grad_fed_all, down_weight, preferred_element_type=jnp.float32
    )
    grad_up = jax.vjp(gelu_exact, up_pre)[1](grad_active)[0].astype(jnp.bfloat16)
    up_bias_grad = jnp.sum(grad_up.astype(jnp.float32), axis=0)
    up_weight_grad = jnp.einsum("td,tf->df", first_all, grad_up, preferred_element_type=jnp.float32)
    grad_first = (
        lax.psum_scatter(
            jnp.einsum("tf,df->td", grad_up, up_weight, preferred_element_type=jnp.float32),
            "tensor",
            scatter_dimension=0,
            tiled=True,
        )
        + grad_second
    )
    grad_res, norm1_gain_grad, norm1_bias_grad = norm_backward(
        grad_first, normed_one, inverse_one, norm1_gain
    )
    grad_att = grad_res.astype(jnp.bfloat16)
    out_bias_grad = jnp.sum(grad_att.astype(jnp.float32), axis=0)
    grad_att_all = lax.all_gather(grad_att, "tensor", axis=0, tiled=True)
    out_weight_grad = jnp.einsum(
        "te,td->ed", context, grad_att_all, preferred_element_type=jnp.float32
    )
    grad_context = jnp.einsum(
        "td,ed->te", grad_att_all, out_weight, preferred_element_type=jnp.float32
    ).astype(jnp.bfloat16)
    grad_queries, grad_keys, grad_values = lax.map(
        attend_backward,
        (
            by_sequence(queries),
            by_sequence(key_rows),
            by_sequence(value_rows),
            segments,
            log_totals,
            by_sequence(grad_context),
        ),
    )
    stacked = jnp.stack(
        [
            grad_queries.reshape(group_rows, local_width),
            grad_keys.reshape(group_rows, local_width),
            grad_values.reshape(group_rows, local_width),
        ]
    )
    qkv_weight_grad = jnp.einsum(
        "td,kte->kde", gathered, stacked, preferred_element_type=jnp.float32
    )
    qv_bias_grad = jnp.stack(
        [
            jnp.sum(stacked[0].astype(jnp.float32), axis=0),
            jnp.sum(stacked[2].astype(jnp.float32), axis=0),
        ]
    )
    input_grad = (
        lax.psum_scatter(
            jnp.einsum(
                "kte,kde->td", stacked, qkv_weight, preferred_element_type=jnp.float32
            ).astype(jnp.bfloat16),
            "tensor",
            scatter_dimension=0,
            tiled=True,
        ).astype(jnp.float32)
        + grad_res
    ).astype(jnp.bfloat16)
    qkv_sum, out_sum, up_sum, down_sum = (
        lax.psum_scatter(qkv_weight_grad, "dp", scatter_dimension=1, tiled=True),
        lax.psum_scatter(out_weight_grad, "dp", scatter_dimension=1, tiled=True),
        lax.psum_scatter(up_weight_grad, "dp", scatter_dimension=0, tiled=True),
        lax.psum_scatter(down_weight_grad, "dp", scatter_dimension=1, tiled=True),
    )
    token_grads = lax.psum(
        (
            out_bias_grad,
            norm1_gain_grad,
            norm1_bias_grad,
            down_bias_grad,
            norm2_gain_grad,
            norm2_bias_grad,
        ),
        ("dp", "tensor"),
    )
    group_grads = lax.psum(
        (
            qv_bias_grad,
            up_bias_grad,
            pool_weight_grad,
            pool_bias_grad,
            class_weight_grad,
            class_bias_grad,
        ),
        "dp",
    )
    return (
        final_norm.astype(jnp.bfloat16),
        input_grad,
        qkv_sum,
        group_grads[0],
        out_sum,
        token_grads[0],
        token_grads[1],
        token_grads[2],
        up_sum,
        group_grads[1],
        down_sum,
        token_grads[3],
        token_grads[4],
        token_grads[5],
        group_grads[2],
        group_grads[3],
        group_grads[4],
        group_grads[5],
    )


def solution(mesh):
    placed = (
        P(("dp", "tensor"), None),
        P("dp", None),
        P("dp"),
        P(None, None, "tensor"),
        P(None, "tensor"),
        P("tensor", None),
        P(),
        P(),
        P(),
        P(None, "tensor"),
        P("tensor"),
        P("tensor", None),
        P(),
        P(),
        P(),
        P(),
        P(),
        P(),
        P(),
        P(("dp", "tensor"), None),
    )
    return jax.shard_map(
        body,
        mesh=mesh,
        in_specs=placed,
        out_specs=(
            P(("dp", "tensor"), None),
            P(("dp", "tensor"), None),
            P(None, "dp", "tensor"),
            P(None, "tensor"),
            P("tensor", "dp"),
            P(),
            P(),
            P(),
            P("dp", "tensor"),
            P("tensor"),
            P("tensor", "dp"),
            P(),
            P(),
            P(),
            P(),
            P(),
            P(),
            P(),
        ),
        check_vma=False,
    )
```

profile of v0, /device:TPU:0, one launch (start us, length us, event | category | flops | bytes accessed | tf_op | source)
XLA Modules:
  0.0 1093.7 jit_solution(14431650405853245202)
XLA Ops:
  8.8 53.6 %all-gather.4.cloned.1.call-done = bf16[1536,768]{1,0:T(8,128)(2,1)} async-done(((bf16[384,768]{1,0:T(8,128)(2,1)}), bf16[1536,768]{1,0:T(8,128)(2,1)}) %all-gather.4.cloned.1.call-update) | async-done | bytes 2359312 | tf_op jit(solution)/shard_map/all_gather | solution.py:120
  76.6 12.6 %while.26 = (s32[]{:T(128)}, bf16[3,512,192]{1,2,0:T(8,128)(2,1)S(1)}, f32[3,3,512]{2,1,0:T(4,128)}, bf16[3,512,192]{1,2,0:T(8,128)(2,1)S(1)}, s32[3,512]{1,0:T(...) while((s32[]{:T(128)}, bf16[3,512,192]{1,2,0:T(8,128)(2,1)S(1)}, ...), condition=%wide.region_3.4_spmd, body=%wide.region_0.3_spmd.sunk | while | flops 211122688 | bytes 12902513 | solution.py:131
  94.9 170.5 %all-reduce.6.cloned.1.call-done = f32[1536,768]{1,0:T(8,128)} async-done(((f32[1536,768]{1,0:T(8,128)}), f32[1536,768]{1,0:T(8,128)}) %all-reduce.6.cloned.1.call-update) | async-done | bytes 4718608 | tf_op jit(solution)/shard_map/psum | solution.py:137
  272.2 13.3 %multiply_convert_fusion = (bf16[1536,768]{1,0:T(8,128)(2,1)S(1)}, f32[1536,768]{1,0:T(8,128)}, f32[1536,768]{1,0:T(8,128)}) fusion(f32[768]{0:T(1024)S(1)} %copy-done.40, bf16[768,768]{1,0:T(8,128)(2,1)S(1)} %copy-done, f32[1536,768]{1,0:T(8,128)S(1)} %subtract_multiply_fusion.1, f32[768]{0:T(1024)S(1)} %copy-done.35, f32[768]{0:T(1024)S(1)} %copy-done.22), kind=kOutput, calls=%fused_computation.53 | convolution fusion | flops 1893335040 | bytes 17703936 | tf_op jit(solution)/shard_map/dot_general | solution.py:146
  286.9 4.2 fusion.93
  291.2 171.0 %all-reduce.8.cloned.1.call-done = f32[1536,768]{1,0:T(8,128)} async-done(((f32[1536,768]{1,0:T(8,128)}), f32[1536,768]{1,0:T(8,128)}) %all-reduce.8.cloned.1.call-update) | async-done | bytes 4718608 | tf_op jit(solution)/shard_map/psum | solution.py:150
  462.2 4.7 fusion.86
  470.8 16.4 %psum.107 = bf16[3,768]{1,0:T(4,128)(2,1)S(1)} all-reduce(f32[3,768]{1,0:T(4,128)S(1)} %fusion.56), channel_id=1, replica_groups=mesh['dp'=8,'tensor'=4] {'tensor'}, use_global_device_ids=true, to_apply=%region_10.11 | all-reduce | flops 2304 | bytes 13824 | tf_op jit(solution)/shard_map/psum | solution.py:163
  496.2 47.9 %all-gather.6.cloned.1.call-done = bf16[1536,768]{1,0:T(8,128)(2,1)} async-done(((bf16[384,768]{1,0:T(8,128)(2,1)}), bf16[1536,768]{1,0:T(8,128)(2,1)}) %all-gather.6.cloned.1.call-update) | async-done | bytes 2359312 | tf_op jit(solution)/shard_map/all_gather | solution.py:194
  544.1 8.8 convert_reduce_fusion
  554.3 4.3 fusion.95
  559.5 83.4 %reduce-scatter.11.cloned.1.call-done = f32[384,768]{1,0:T(8,128)} async-done(((f32[1536,768]{1,0:T(8,128)}), f32[384,768]{1,0:T(8,128)}) %reduce-scatter.11.cloned.1.call-update) | async-done | bytes 1179664 | tf_op jit(solution)/shard_map/reduce_scatter | solution.py:205
  651.2 50.4 %all-gather.8.cloned.1.call-done = bf16[1536,768]{1,0:T(8,128)(2,1)} async-done(((bf16[384,768]{1,0:T(8,128)(2,1)}), bf16[1536,768]{1,0:T(8,128)(2,1)}) %all-gather.8.cloned.1.call-update) | async-done | bytes 2359312 | tf_op jit(solution)/shard_map/all_gather | solution.py:218
  706.1 75.7 %while.27 = (s32[]{:T(128)}, bf16[3,512,192]{1,2,0:T(8,128)(2,1)S(1)}, bf16[3,512,192]{1,2,0:T(8,128)(2,1)}, bf16[3,512,192]{1,2,0:T(8,128)(2,1)S(1)}, bf16[3,51...) while((s32[]{:T(128)}, ...), condition=%wide.region_20.21_spmd, body=%wide.region_18.20_spmd.sunk | while | flops 515084288 | bytes 27811988 | solution.py:225
  716.5 5.8 fusion.176
  724.8 5.8 fusion.178
  741.7 5.8 fusion.176
  750.0 5.8 fusion.178
  767.0 5.8 fusion.176
  775.3 5.8 fusion.178
  801.4 4.3 fusion.49
  805.7 4.2 copy.87
  809.9 4.8 reshape.315
  815.0 4.6 bitcast_convert_fusion
  821.7 6.6 fusion.58
  828.5 5.9 fusion.96
  836.0 40.0 %all-reduce = (f32[768]{0:T(1024)}, f32[768]{0:T(1024)}, f32[768]{0:T(1024)}, f32[768]{0:T(1024)}, f32[768]{0:T(1024)}, /*index=5*/f32[768]{0:T(1024)}) all-reduce(f32[768]{0:T(1024)} %get-tuple-element.275, f32[768]{0:T(1024)} %get-tuple-element.222, ...), channel_id=1, replica_groups=mesh['dp'=8,'tensor'=4] {'dp','tensor'}, use_global_device_ids=true, to_apply=%region_28.29 | all-reduce | flops 4608 | bytes 36864 | tf_op jit(solution)/shard_map/psum | solution.py:269
  876.3 25.2 %all-reduce.1 = (f32[2,192]{1,0:T(2,128)}, f32[768]{0:T(1024)}, f32[768]{0:T(1024)}, f32[768,3]{0,1:T(4,128)}, f32[3]{0:T(128)}) all-reduce(f32[2,192]{1,0:T(2,128)S(1)} %pad_maximum_fusion, f32[768]{0:T(1024)} %get-tuple-element.279, f32[768]{0:T(1024)} %get-tuple-element.301, ...), channel_id=1, replica_groups=mesh['dp'=8,'tensor'=4] {'dp'}, use_global_device_ids=true, to_apply=%region_25.26 | all-reduce | flops 4227 | bytes 33816 | tf_op jit(solution)/shard_map/psum | solution.py:280
  905.0 21.0 %reduce-scatter.13.cloned.1.call-done = bf16[384,768]{1,0:T(8,128)(2,1)} async-done(((bf16[1536,768]{1,0:T(8,128)(2,1)}), bf16[384,768]{1,0:T(8,128)(2,1)}) %reduce-scatter.13.cloned.1.call-update) | async-done | bytes 589840 | tf_op jit(solution)/shard_map/reduce_scatter | solution.py:253
  928.7 62.9 %all-reduce.10.cloned.1.call-done = f32[768,768]{1,0:T(8,128)} async-done(((f32[768,768]{1,0:T(8,128)}), f32[768,768]{1,0:T(8,128)}) %all-reduce.10.cloned.1.call-update) | async-done | bytes 2359312 | tf_op jit(solution)/shard_map/psum | solution.py:280
  991.6 45.7 %reduce-scatter.15.cloned.1.call-done = f32[96,768]{1,0:T(8,128)} async-done(((f32[768,768]{1,0:T(8,128)}), f32[96,768]{1,0:T(8,128)}) %reduce-scatter.15.cloned.1.call-update) | async-done | bytes 294928 | tf_op jit(solution)/shard_map/reduce_scatter | solution.py:266
  1037.2 46.2 %reduce-scatter.17.cloned.1.call-done = f32[768,96]{0,1:T(8,128)} async-done(((f32[768,768]{0,1:T(8,128)}), f32[768,96]{0,1:T(8,128)}) %reduce-scatter.17.cloned.1.call-update) | async-done | bytes 294928 | tf_op jit(solution)/shard_map/reduce_scatter | solution.py:267
  (247 shorter events, 143.9 us)
Async XLA Ops:
  7.2 265.0 %copy-start = (bf16[768,768]{1,0:T(8,128)(2,1)S(1)}, bf16[768,768]{1,0:T(8,128)(2,1)}, u32[]{:S(2)}) copy-start(bf16[768,768]{1,0:T(8,128)(2,1)} %param.33) | copy-start | bytes 3538948
  7.2 55.1 %all-gather.4.cloned.1.call-start = ((), (), s32[]{:S(2)}) async-start(), calls=%async_computation.6 | async-start | bytes 2949120 | tf_op jit(solution)/shard_map/all_gather | solution.py:120
  7.9 257.5 %all-reduce.6.cloned.1.call-start = ((), (), s32[]{:S(2)}) async-start(), calls=%async_computation.7 | async-start | bytes 9437184 | tf_op jit(solution)/shard_map/psum | solution.py:137
  94.5 170.9 %copy-start.3 = (bf16[1536,768]{1,0:T(8,128)(2,1)S(1)}, bf16[1536,768]{1,0:T(8,128)(2,1)}, u32[]{:S(2)}) copy-start(bf16[1536,768]{1,0:T(8,128)(2,1)} %all-gather.4.cloned.1.call-done) | copy-start | bytes 7077892
  94.5 170.9 %copy-start.26 = (f32[768]{0:T(1024)S(1)}, f32[768]{0:T(1024)}, u32[]{:S(2)}) copy-start(f32[768]{0:T(1024)} %param.30) | copy-start | bytes 9220
  94.5 367.7 %all-reduce.8.cloned.1.call-start = ((), (), s32[]{:S(2)}) async-start(), calls=%async_computation.8 | async-start | bytes 9437184 | tf_op jit(solution)/shard_map/psum | solution.py:150
  272.2 13.3 %copy-start.2 = (f32[1536,768]{1,0:T(8,128)}, f32[1536,768]{1,0:T(8,128)S(1)}, u32[]{:S(2)}) copy-start(f32[1536,768]{1,0:T(8,128)S(1)} %subtract_multiply_fusion.1) | copy-start | bytes 14155780
  272.2 14.7 %copy-start.38 = (bf16[768,768]{1,0:T(8,128)(2,1)S(1)}, bf16[768,768]{1,0:T(8,128)(2,1)}, u32[]{:S(2)}) copy-start(bf16[768,768]{1,0:T(8,128)(2,1)} %param.35) | copy-start | bytes 3538948
  291.1 171.1 %copy-start.33 = (f32[768]{0:T(1024)S(1)}, f32[768]{0:T(1024)}, u32[]{:S(2)}) copy-start(f32[768]{0:T(1024)} %param.36) | copy-start | bytes 9220
  291.1 253.0 %all-gather.6.cloned.1.call-start = ((), (), s32[]{:S(2)}) async-start(), calls=%async_computation.9 | async-start | bytes 2949120 | tf_op jit(solution)/shard_map/all_gather | solution.py:194
  467.6 19.7 %copy-start.16 = (bf16[768,768]{1,0:T(8,128)(2,1)S(1)}, bf16[768,768]{1,0:T(8,128)(2,1)}, u32[]{:S(2)}) copy-start(bf16[768,768]{1,0:T(8,128)(2,1)} %param.39) | copy-start | bytes 3538948
  467.6 19.7 %copy-start.34 = (f32[768]{0:T(1024)S(1)}, f32[768]{0:T(1024)}, u32[]{:S(2)}) copy-start(f32[768]{0:T(1024)} %param.40) | copy-start | bytes 9220
  467.6 19.9 %copy-start.39 = (bf16[768,3]{0,1:T(4,128)(2,1)S(1)}, bf16[768,3]{0,1:T(4,128)(2,1)}, u32[]{:S(2)}) copy-start(bf16[768,3]{0,1:T(4,128)(2,1)} %param.41) | copy-start | bytes 13828
  467.6 19.9 %copy-start.42 = (f32[3]{0:T(128)S(1)}, f32[3]{0:T(128)}, u32[]{:S(2)}) copy-start(f32[3]{0:T(128)} %param.42) | copy-start | bytes 40
  467.6 20.1 %copy-start.37 = (s32[3]{0:T(128)S(1)}, s32[3]{0:T(128)}, u32[]{:S(2)}) copy-start(s32[3]{0:T(128)} %param.26) | copy-start | bytes 40
  468.1 21.4 %copy-start.18 = (bf16[384,768]{1,0:T(8,128)(2,1)S(1)}, bf16[384,768]{1,0:T(8,128)(2,1)}, u32[]{:S(2)}) copy-start(bf16[384,768]{1,0:T(8,128)(2,1)} %param.43) | copy-start | bytes 1769476
  489.6 54.5 %copy-start.41 = (f32[768]{0:T(1024)S(1)}, f32[768]{0:T(1024)}, u32[]{:S(2)}) copy-start(f32[768]{0:T(1024)} %param.34) | copy-start | bytes 9220
  495.6 147.2 %reduce-scatter.11.cloned.1.call-start = ((), (), s32[]{:S(2)}) async-start(), calls=%async_computation.10 | async-start | bytes 5898240 | tf_op jit(solution)/shard_map/reduce_scatter | solution.py:205
  558.6 143.0 %all-gather.8.cloned.1.call-start = ((), (), s32[]{:S(2)}) async-start(), calls=%async_computation.11 | async-start | bytes 2949120 | tf_op jit(solution)/shard_map/all_gather | solution.py:218
  559.4 87.5 %copy-start.29 = (f32[384]{0:T(512)}, f32[384]{0:T(512)S(1)}, u32[]{:S(2)}) copy-start(f32[384]{0:T(512)S(1)} %dynamic-slice.6) | copy-start | bytes 4612
  646.9 54.7 %copy-start.19 = (bf16[192,768]{1,0:T(8,128)(2,1)S(1)}, bf16[192,768]{1,0:T(8,128)(2,1)}, u32[]{:S(2)}) copy-start(bf16[192,768]{1,0:T(8,128)(2,1)} %param.29) | copy-start | bytes 884740
  647.0 57.3 %copy-start.30 = (f32[384]{0:T(512)}, f32[384]{0:T(512)S(1)}, u32[]{:S(2)}) copy-start(f32[384]{0:T(512)S(1)} %broadcast_multiply_fusion.2) | copy-start | bytes 4612
  647.0 57.3 %copy-start.31 = (f32[384]{0:T(512)}, f32[384]{0:T(512)S(1)}, u32[]{:S(2)}) copy-start(f32[384]{0:T(512)S(1)} %broadcast_multiply_fusion.3) | copy-start | bytes 4612
  651.0 250.5 %reduce-scatter.21.cloned.1.call-start = ((), (), s32[]{:S(2)}) async-start(), calls=%async_computation.17 | async-start | bytes 884736
  797.5 105.6 %reduce-scatter.19.cloned.1.call-start = ((), (), s32[]{:S(2)}) async-start(), calls=%async_computation.16 | async-start | bytes 2211840
  814.7 111.3 %reduce-scatter.13.cloned.1.call-start = ((), (), s32[]{:S(2)}) async-start(), calls=%async_computation.12 | async-start | bytes 2949120 | tf_op jit(solution)/shard_map/reduce_scatter | solution.py:253
  819.6 171.9 %all-reduce.10.cloned.1.call-start = ((), (), s32[]{:S(2)}) async-start(), calls=%async_computation.15 | async-start | bytes 4718592 | tf_op jit(solution)/shard_map/psum | solution.py:280
  821.7 215.5 %reduce-scatter.15.cloned.1.call-start = ((), (), s32[]{:S(2)}) async-start(), calls=%async_computation.13 | async-start | bytes 2654208 | tf_op jit(solution)/shard_map/reduce_scatter | solution.py:266
  828.4 47.6 %copy-start.14 = (bf16[3,512,192]{1,2,0:T(8,128)(2,1)S(1)}, bf16[3,512,192]{1,2,0:T(8,128)(2,1)}, u32[]{:S(2)}) copy-start(bf16[3,512,192]{1,2,0:T(8,128)(2,1)} %copy-done.13) | copy-start | bytes 1769476
  828.4 254.9 %reduce-scatter.17.cloned.1.call-start = ((), (), s32[]{:S(2)}) async-start(), calls=%async_computation.14 | async-start | bytes 2654208 | tf_op jit(solution)/shard_map/reduce_scatter | solution.py:267
  834.4 41.7 %copy-start.12 = (bf16[3,512,192]{1,2,0:T(8,128)(2,1)S(1)}, bf16[3,512,192]{1,2,0:T(8,128)(2,1)}, u32[]{:S(2)}) copy-start(bf16[3,512,192]{1,2,0:T(8,128)(2,1)} %copy-done.11) | copy-start | bytes 1769476
  834.4 91.7 %copy-start.10 = (f32[384,768]{1,0:T(8,128)S(1)}, f32[384,768]{1,0:T(8,128)}, u32[]{:S(2)}) copy-start(f32[384,768]{1,0:T(8,128)} %copy-done.9) | copy-start | bytes 3538948
  (25 other events, 82.0 us)
Sparse Core Ops, SparseCore 0:
  9.6 52.6 all-gather.3
  94.7 170.7 all-reduce.5
  291.2 170.9 all-reduce.7
  495.7 48.3 all-gather.5
  558.7 84.0 reduce-scatter.10
  651.1 50.4 all-gather.7
  797.7 33.6 reduce-scatter.20
  834.8 40.5 reduce-scatter.18
  878.3 47.6 reduce-scatter.12
  929.2 62.3 all-reduce.9
  995.5 41.6 reduce-scatter.14
  1041.0 42.3 reduce-scatter.16
where the time goes:
time: 1100 us; the launch traced here: 1090 us
  waiting for transfers between devices  753 us (68%)
  matrix products  137 us (12%)
  blocking collectives  81.6 us (7%)
  local copies, waits for them, and re-layouts  73.4 us (7%)
  other arithmetic  31 us (3%)
  between operations  15 us (1%)
    psum x1, waiting for transfers between devices, body(): lax.psum(jnp.dot(active, down_weight, preferred_element_type=jnp.float32)...  171 us
    psum x1, waiting for transfers between devices, body(): lax.psum(jnp.dot(context, out_weight, preferred_element_type=jnp.float32)...  171 us
    reduce_scatter x1, waiting for transfers between devices, body(): lax.psum_scatter(jnp.einsum('tf,df->td', grad_up, up_weight, preferred_el...  83.4 us
    psum x1, waiting for transfers between devices, body(): lax.psum((qv_bias_grad, up_bias_grad, pool_weight_grad, pool_bias_grad, c...  62.9 us
    all_gather x1, waiting for transfers between devices, body(): gathered = lax.all_gather(inputs, 'tensor', axis=0, tiled=True)  53.6 us
    all_gather x1, waiting for transfers between devices, body(): grad_att_all = lax.all_gather(grad_att, 'tensor', axis=0, tiled=True)  50.4 us
    all_gather x1, waiting for transfers between devices, body(): grad_fed_all = lax.all_gather(grad_fed, 'tensor', axis=0, tiled=True)  47.9 us
    reduce_scatter x1, waiting for transfers between devices, body(): lax.psum_scatter(down_weight_grad, 'dp', scatter_dimension=1, tiled=True)  46.2 us
  transfers between devices with their start and end apart: 12, of which 10 were waited for; matrix products, arithmetic and copies ran while one was open for 4% of the time, Pallas kernels for 0%

commit v1 on v0

--- a/solution.py
+++ b/solution.py
@@ -7,6 +7,19 @@
 HEAD = 64
 epsilon = 1e-12
 masked_value = -1e30
+
+
+def ring_gather(value, axis, dim):
+    count, index, extent = (lax.axis_size(axis), lax.axis_index(axis), value.shape[dim])
+    right = [(i, (i + 1) % count) for i in range(count)]
+    whole = jnp.zeros((*value.shape[:dim], count * extent, *value.shape[dim + 1 :]), value.dtype)
+    held = value
+    for hop in range(count):
+        holder = (index - hop) % count
+        whole = lax.dynamic_update_slice_in_dim(whole, held, holder * extent, axis=dim)
+        if hop < count - 1:
+            held = lax.ppermute(held, axis, right)
+    return whole
 
 
 def norm_forward(values, norm_gain, norm_shift):
@@ -215,7 +228,7 @@
     )
     grad_att = grad_res.astype(jnp.bfloat16)
     out_bias_grad = jnp.sum(grad_att.astype(jnp.float32), axis=0)
-    grad_att_all = lax.all_gather(grad_att, "tensor", axis=0, tiled=True)
+    grad_att_all = ring_gather(grad_att, "tensor", 0)
     out_weight_grad = jnp.einsum(
         "te,td->ed", context, grad_att_all, preferred_element_type=jnp.float32
     )

time: 1100 us -> 1100 us (level)
    all_gather x1 -> x0, waiting for transfers between devices: 50.4 us -> none  [body(): grad_att_all = lax.all_gather(grad_att, 'tensor', axis=0, tiled=True)]
    ppermute x0 -> x3, waiting for transfers between devices: none -> 45.9 us  [ring_gather(): held = lax.ppermute(held, axis, right)]
    unnamed x98 -> x100, local copies, waits for them, and re-layouts: 28.1 us -> 28.3 us
  transfers between devices with their start and end apart: 12 -> 14, of which waited for: 10 -> 12; matrix products, arithmetic and copies ran while one was open for 4% -> 4% of each run, Pallas kernels for 0% -> 0%
where the time goes in v1:
time: 1100 us; the launch traced here: 1090 us
  waiting for transfers between devices  750 us (68%)
  matrix products  134 us (12%)
  blocking collectives  80 us (7%)
  local copies, waits for them, and re-layouts  77 us (7%)
  other arithmetic  30.2 us (3%)
  between operations  14.7 us (1%)
    psum x1, waiting for transfers between devices, body(): lax.psum(jnp.dot(active, down_weight, preferred_element_type=jnp.float32)...  171 us
    psum x1, waiting for transfers between devices, body(): lax.psum(jnp.dot(context, out_weight, preferred_element_type=jnp.float32)...  171 us
    reduce_scatter x1, waiting for transfers between devices, body(): lax.psum_scatter(jnp.einsum('tf,df->td', grad_up, up_weight, preferred_el...  83.4 us
    psum x1, waiting for transfers between devices, body(): lax.psum((qv_bias_grad, up_bias_grad, pool_weight_grad, pool_bias_grad, c...  63 us
    all_gather x1, waiting for transfers between devices, body(): gathered = lax.all_gather(inputs, 'tensor', axis=0, tiled=True)  53.6 us
    all_gather x1, waiting for transfers between devices, body(): grad_fed_all = lax.all_gather(grad_fed, 'tensor', axis=0, tiled=True)  48.2 us
    reduce_scatter x1, waiting for transfers between devices, body(): lax.psum_scatter(down_weight_grad, 'dp', scatter_dimension=1, tiled=True)  46.3 us
    ppermute x3, waiting for transfers between devices, ring_gather(): held = lax.ppermute(held, axis, right)  45.9 us
  transfers between devices with their start and end apart: 14, of which 12 were waited for; matrix products, arithmetic and copies ran while one was open for 4% of the time, Pallas kernels for 0%

profile of v1, /device:TPU:0, one launch (start us, length us, event | category | flops | bytes accessed | tf_op | source)
XLA Modules:
  0.0 1089.1 jit_solution(9138317968665860672)
XLA Ops:
  8.8 53.6 %all-gather.3.cloned.1.call-done = bf16[1536,768]{1,0:T(8,128)(2,1)} async-done(((bf16[384,768]{1,0:T(8,128)(2,1)}), bf16[1536,768]{1,0:T(8,128)(2,1)}) %all-gather.3.cloned.1.call-update) | async-done | bytes 2359312 | tf_op jit(solution)/shard_map/all_gather | solution.py:133
  76.6 12.6 %while.26 = (s32[]{:T(128)}, bf16[3,512,192]{1,2,0:T(8,128)(2,1)S(1)}, f32[3,3,512]{2,1,0:T(4,128)}, bf16[3,512,192]{1,2,0:T(8,128)(2,1)S(1)}, s32[3,512]{1,0:T(...) while((s32[]{:T(128)}, bf16[3,512,192]{1,2,0:T(8,128)(2,1)S(1)}, ...), condition=%wide.region_3.4_spmd, body=%wide.region_0.3_spmd.sunk | while | flops 211122688 | bytes 12902513 | solution.py:144
  94.8 170.7 %all-reduce.6.cloned.1.call-done = f32[1536,768]{1,0:T(8,128)} async-done(((f32[1536,768]{1,0:T(8,128)}), f32[1536,768]{1,0:T(8,128)}) %all-reduce.6.cloned.1.call-update) | async-done | bytes 4718608 | tf_op jit(solution)/shard_map/psum | solution.py:150
  272.2 13.3 %multiply_convert_fusion = (bf16[1536,768]{1,0:T(8,128)(2,1)S(1)}, f32[1536,768]{1,0:T(8,128)}, f32[1536,768]{1,0:T(8,128)}) fusion(f32[768]{0:T(1024)S(1)} %copy-done.41, bf16[768,768]{1,0:T(8,128)(2,1)S(1)} %copy-done, f32[1536,768]{1,0:T(8,128)S(1)} %subtract_multiply_fusion.1, f32[768]{0:T(1024)S(1)} %copy-done.36, f32[768]{0:T(1024)S(1)} %copy-done.23), kind=kOutput, calls=%fused_computation.53 | convolution fusion | flops 1893335040 | bytes 17703936 | tf_op jit(solution)/shard_map/dot_general | solution.py:159
  291.2 171.0 %all-reduce.8.cloned.1.call-done = f32[1536,768]{1,0:T(8,128)} async-done(((f32[1536,768]{1,0:T(8,128)}), f32[1536,768]{1,0:T(8,128)}) %all-reduce.8.cloned.1.call-update) | async-done | bytes 4718608 | tf_op jit(solution)/shard_map/psum | solution.py:163
  462.2 4.7 fusion.86
  470.9 16.4 %psum.107 = bf16[3,768]{1,0:T(4,128)(2,1)S(1)} all-reduce(f32[3,768]{1,0:T(4,128)S(1)} %fusion.56), channel_id=1, replica_groups=mesh['dp'=8,'tensor'=4] {'tensor'}, use_global_device_ids=true, to_apply=%region_10.11 | all-reduce | flops 2304 | bytes 13824 | tf_op jit(solution)/shard_map/psum | solution.py:176
  495.9 48.2 %all-gather.5.cloned.1.call-done = bf16[1536,768]{1,0:T(8,128)(2,1)} async-done(((bf16[384,768]{1,0:T(8,128)(2,1)}), bf16[1536,768]{1,0:T(8,128)(2,1)}) %all-gather.5.cloned.1.call-update) | async-done | bytes 2359312 | tf_op jit(solution)/shard_map/all_gather | solution.py:207
  544.1 8.8 convert_reduce_fusion
  554.3 4.3 fusion.95
  559.5 83.4 %reduce-scatter.11.cloned.1.call-done = f32[384,768]{1,0:T(8,128)} async-done(((f32[1536,768]{1,0:T(8,128)}), f32[384,768]{1,0:T(8,128)}) %reduce-scatter.11.cloned.1.call-update) | async-done | bytes 1179664 | tf_op jit(solution)/shard_map/reduce_scatter | solution.py:218
  651.7 15.3 %collective-permute-done = bf16[384,768]{1,0:T(8,128)(2,1)S(1)} collective-permute-done((bf16[384,768]{1,0:T(8,128)(2,1)S(1)}, bf16[384,768]{1,0:T(8,128)(2,1)S(1)}, u32[]{:S(2)}, u32[]{:S(2)}) %collective-permute-start) | collective-permute-done | bytes 589856 | tf_op jit(solution)/shard_map/ppermute | solution.py:21
  667.0 15.9 %collective-permute-done.1 = bf16[384,768]{1,0:T(8,128)(2,1)S(1)} collective-permute-done((bf16[384,768]{1,0:T(8,128)(2,1)S(1)}, bf16[384,768]{1,0:T(8,128)(2,1)S(1)}, u32[]{:S(2)}, u32[]{:S(2)}) %collective-permute-start.1) | collective-permute-done | bytes 589856 | tf_op jit(solution)/shard_map/ppermute | solution.py:21
  683.8 14.7 %collective-permute-done.2 = bf16[384,768]{1,0:T(8,128)(2,1)S(1)} collective-permute-done((bf16[384,768]{1,0:T(8,128)(2,1)S(1)}, bf16[384,768]{1,0:T(8,128)(2,1)S(1)}, u32[]{:S(2)}, u32[]{:S(2)}) %collective-permute-start.2) | collective-permute-done | bytes 589856 | tf_op jit(solution)/shard_map/ppermute | solution.py:21
  703.4 75.7 %while.27 = (s32[]{:T(128)}, bf16[3,512,192]{1,2,0:T(8,128)(2,1)S(1)}, bf16[3,512,192]{1,2,0:T(8,128)(2,1)}, bf16[3,512,192]{1,2,0:T(8,128)(2,1)S(1)}, bf16[3,51...) while((s32[]{:T(128)}, ...), condition=%wide.region_20.21_spmd, body=%wide.region_18.20_spmd.sunk | while | flops 515084288 | bytes 27811988 | solution.py:238
  713.8 5.8 fusion.176
  722.1 5.8 fusion.178
  739.0 5.8 fusion.176
  747.3 5.8 fusion.178
  764.2 5.8 fusion.176
  772.5 5.8 fusion.178
  797.8 4.3 fusion.49
  806.3 4.8 reshape.315
  811.4 4.7 bitcast_convert_fusion
  818.2 6.6 fusion.58
  824.9 6.0 fusion.96
  832.5 38.8 %all-reduce = (f32[768]{0:T(1024)}, f32[768]{0:T(1024)}, f32[768]{0:T(1024)}, f32[768]{0:T(1024)}, f32[768]{0:T(1024)}, /*index=5*/f32[768]{0:T(1024)}) all-reduce(f32[768]{0:T(1024)} %get-tuple-element.275, f32[768]{0:T(1024)} %get-tuple-element.222, ...), channel_id=1, replica_groups=mesh['dp'=8,'tensor'=4] {'dp','tensor'}, use_global_device_ids=true, to_apply=%region_28.29 | all-reduce | flops 4608 | bytes 36864 | tf_op jit(solution)/shard_map/psum | solution.py:282
  871.6 24.8 %all-reduce.1 = (f32[2,192]{1,0:T(2,128)}, f32[768]{0:T(1024)}, f32[768]{0:T(1024)}, f32[768,3]{0,1:T(4,128)}, f32[3]{0:T(128)}) all-reduce(f32[2,192]{1,0:T(2,128)S(1)} %pad_maximum_fusion, f32[768]{0:T(1024)} %get-tuple-element.279, f32[768]{0:T(1024)} %get-tuple-element.301, ...), channel_id=1, replica_groups=mesh['dp'=8,'tensor'=4] {'dp'}, use_global_device_ids=true, to_apply=%region_25.26 | all-reduce | flops 4227 | bytes 33816 | tf_op jit(solution)/shard_map/psum | solution.py:293
  899.9 21.8 %reduce-scatter.13.cloned.1.call-done = bf16[384,768]{1,0:T(8,128)(2,1)} async-done(((bf16[1536,768]{1,0:T(8,128)(2,1)}), bf16[384,768]{1,0:T(8,128)(2,1)}) %reduce-scatter.13.cloned.1.call-update) | async-done | bytes 589840 | tf_op jit(solution)/shard_map/reduce_scatter | solution.py:266
  924.4 63.0 %all-reduce.10.cloned.1.call-done = f32[768,768]{1,0:T(8,128)} async-done(((f32[768,768]{1,0:T(8,128)}), f32[768,768]{1,0:T(8,128)}) %all-reduce.10.cloned.1.call-update) | async-done | bytes 2359312 | tf_op jit(solution)/shard_map/psum | solution.py:293
  987.4 45.5 %reduce-scatter.15.cloned.1.call-done = f32[96,768]{1,0:T(8,128)} async-done(((f32[768,768]{1,0:T(8,128)}), f32[96,768]{1,0:T(8,128)}) %reduce-scatter.15.cloned.1.call-update) | async-done | bytes 294928 | tf_op jit(solution)/shard_map/reduce_scatter | solution.py:279
  1032.9 46.3 %reduce-scatter.17.cloned.1.call-done = f32[768,96]{0,1:T(8,128)} async-done(((f32[768,768]{0,1:T(8,128)}), f32[768,96]{0,1:T(8,128)}) %reduce-scatter.17.cloned.1.call-update) | async-done | bytes 294928 | tf_op jit(solution)/shard_map/reduce_scatter | solution.py:280
  (257 shorter events, 152.6 us)
Async XLA Ops:
  7.2 265.0 %copy-start = (bf16[768,768]{1,0:T(8,128)(2,1)S(1)}, bf16[768,768]{1,0:T(8,128)(2,1)}, u32[]{:S(2)}) copy-start(bf16[768,768]{1,0:T(8,128)(2,1)} %param.33) | copy-start | bytes 3538948
  7.2 55.1 %all-gather.3.cloned.1.call-start = ((), (), s32[]{:S(2)}) async-start(), calls=%async_computation.6 | async-start | bytes 2949120 | tf_op jit(solution)/shard_map/all_gather | solution.py:133
  7.9 257.5 %all-reduce.6.cloned.1.call-start = ((), (), s32[]{:S(2)}) async-start(), calls=%async_computation.7 | async-start | bytes 9437184 | tf_op jit(solution)/shard_map/psum | solution.py:150
  94.5 170.9 %copy-start.3 = (bf16[1536,768]{1,0:T(8,128)(2,1)S(1)}, bf16[1536,768]{1,0:T(8,128)(2,1)}, u32[]{:S(2)}) copy-start(bf16[1536,768]{1,0:T(8,128)(2,1)} %all-gather.3.cloned.1.call-done) | copy-start | bytes 7077892
  94.5 170.9 %copy-start.27 = (f32[768]{0:T(1024)S(1)}, f32[768]{0:T(1024)}, u32[]{:S(2)}) copy-start(f32[768]{0:T(1024)} %param.30) | copy-start | bytes 9220
  94.6 367.7 %all-reduce.8.cloned.1.call-start = ((), (), s32[]{:S(2)}) async-start(), calls=%async_computation.8 | async-start | bytes 9437184 | tf_op jit(solution)/shard_map/psum | solution.py:163
  291.1 171.1 %copy-start.34 = (f32[768]{0:T(1024)S(1)}, f32[768]{0:T(1024)}, u32[]{:S(2)}) copy-start(f32[768]{0:T(1024)} %param.36) | copy-start | bytes 9220
  291.2 253.0 %all-gather.5.cloned.1.call-start = ((), (), s32[]{:S(2)}) async-start(), calls=%async_computation.9 | async-start | bytes 2949120 | tf_op jit(solution)/shard_map/all_gather | solution.py:207
  467.6 19.7 %copy-start.17 = (bf16[768,768]{1,0:T(8,128)(2,1)S(1)}, bf16[768,768]{1,0:T(8,128)(2,1)}, u32[]{:S(2)}) copy-start(bf16[768,768]{1,0:T(8,128)(2,1)} %param.39) | copy-start | bytes 3538948
  467.6 19.7 %copy-start.35 = (f32[768]{0:T(1024)S(1)}, f32[768]{0:T(1024)}, u32[]{:S(2)}) copy-start(f32[768]{0:T(1024)} %param.40) | copy-start | bytes 9220
  467.6 19.9 %copy-start.40 = (bf16[768,3]{0,1:T(4,128)(2,1)S(1)}, bf16[768,3]{0,1:T(4,128)(2,1)}, u32[]{:S(2)}) copy-start(bf16[768,3]{0,1:T(4,128)(2,1)} %param.41) | copy-start | bytes 13828
  467.6 19.9 %copy-start.43 = (f32[3]{0:T(128)S(1)}, f32[3]{0:T(128)}, u32[]{:S(2)}) copy-start(f32[3]{0:T(128)} %param.42) | copy-start | bytes 40
  467.7 20.1 %copy-start.38 = (s32[3]{0:T(128)S(1)}, s32[3]{0:T(128)}, u32[]{:S(2)}) copy-start(s32[3]{0:T(128)} %param.26) | copy-start | bytes 40
  468.2 21.4 %copy-start.19 = (bf16[384,768]{1,0:T(8,128)(2,1)S(1)}, bf16[384,768]{1,0:T(8,128)(2,1)}, u32[]{:S(2)}) copy-start(bf16[384,768]{1,0:T(8,128)(2,1)} %param.43) | copy-start | bytes 1769476
  489.6 54.5 %copy-start.42 = (f32[768]{0:T(1024)S(1)}, f32[768]{0:T(1024)}, u32[]{:S(2)}) copy-start(f32[768]{0:T(1024)} %param.34) | copy-start | bytes 9220
  495.6 147.2 %reduce-scatter.11.cloned.1.call-start = ((), (), s32[]{:S(2)}) async-start(), calls=%async_computation.10 | async-start | bytes 5898240 | tf_op jit(solution)/shard_map/reduce_scatter | solution.py:218
  558.7 337.7 %reduce-scatter.21.cloned.1.call-start = ((), (), s32[]{:S(2)}) async-start(), calls=%async_computation.16 | async-start | bytes 884736
  559.5 87.5 %copy-start.30 = (f32[384]{0:T(512)}, f32[384]{0:T(512)S(1)}, u32[]{:S(2)}) copy-start(f32[384]{0:T(512)S(1)} %dynamic-slice.6) | copy-start | bytes 4612
  647.0 20.0 %copy-start.31 = (f32[384]{0:T(512)}, f32[384]{0:T(512)S(1)}, u32[]{:S(2)}) copy-start(f32[384]{0:T(512)S(1)} %broadcast_multiply_fusion.2) | copy-start | bytes 4612
  647.0 20.0 %copy-start.32 = (f32[384]{0:T(512)}, f32[384]{0:T(512)S(1)}, u32[]{:S(2)}) copy-start(f32[384]{0:T(512)S(1)} %broadcast_multiply_fusion.3) | copy-start | bytes 4612
  650.2 16.8 %collective-permute-start = (bf16[384,768]{1,0:T(8,128)(2,1)S(1)}, bf16[384,768]{1,0:T(8,128)(2,1)S(1)}, u32[]{:S(2)}, u32[]{:S(2)}) collective-permute-start(bf16[384,768]{1,0:T(8,128)(2,1)S(1)} %get-tuple-element.276), channel_id=1, source_target_pairs={{0,1},{1,2},{2,3},{3,0},{4,5},{5,6},{6,7},{7,4},{8,9},{9,10},{10,1... | collective-permute-start | bytes 1769480 | tf_op jit(solution)/shard_map/ppermute | solution.py:21
  667.0 16.0 %collective-permute-start.1 = (bf16[384,768]{1,0:T(8,128)(2,1)S(1)}, bf16[384,768]{1,0:T(8,128)(2,1)S(1)}, u32[]{:S(2)}, u32[]{:S(2)}) collective-permute-start(bf16[384,768]{1,0:T(8,128)(2,1)S(1)} %collective-permute-done), channel_id=1, source_target_pairs={{0,1},{1,2},{2,3},{3,0},{4,5},{5,6},{6,7},{7,4},{8,9},{9,10},{10,1... | collective-permute-start | bytes 1769480 | tf_op jit(solution)/shard_map/ppermute | solution.py:21
  682.9 15.5 %collective-permute-start.2 = (bf16[384,768]{1,0:T(8,128)(2,1)S(1)}, bf16[384,768]{1,0:T(8,128)(2,1)S(1)}, u32[]{:S(2)}, u32[]{:S(2)}) collective-permute-start(bf16[384,768]{1,0:T(8,128)(2,1)S(1)} %collective-permute-done.1), channel_id=1, source_target_pairs={{0,1},{1,2},{2,3},{3,0},{4,5},{5,6},{6,7},{7,4},{8,9},{9,10},{10,1... | collective-permute-start | bytes 1769480 | tf_op jit(solution)/shard_map/ppermute | solution.py:21
  683.4 15.1 %copy-start.20 = (bf16[192,768]{1,0:T(8,128)(2,1)S(1)}, bf16[192,768]{1,0:T(8,128)(2,1)}, u32[]{:S(2)}) copy-start(bf16[192,768]{1,0:T(8,128)(2,1)} %param.29) | copy-start | bytes 884740
  793.9 104.1 %reduce-scatter.19.cloned.1.call-start = ((), (), s32[]{:S(2)}) async-start(), calls=%async_computation.15 | async-start | bytes 2211840
  811.2 110.6 %reduce-scatter.13.cloned.1.call-start = ((), (), s32[]{:S(2)}) async-start(), calls=%async_computation.11 | async-start | bytes 2949120 | tf_op jit(solution)/shard_map/reduce_scatter | solution.py:266
  816.1 171.3 %all-reduce.10.cloned.1.call-start = ((), (), s32[]{:S(2)}) async-start(), calls=%async_computation.14 | async-start | bytes 4718592 | tf_op jit(solution)/shard_map/psum | solution.py:293
  818.2 214.7 %reduce-scatter.15.cloned.1.call-start = ((), (), s32[]{:S(2)}) async-start(), calls=%async_computation.12 | async-start | bytes 2654208 | tf_op jit(solution)/shard_map/reduce_scatter | solution.py:279
  824.9 46.4 %copy-start.14 = (bf16[3,512,192]{1,2,0:T(8,128)(2,1)S(1)}, bf16[3,512,192]{1,2,0:T(8,128)(2,1)}, u32[]{:S(2)}) copy-start(bf16[3,512,192]{1,2,0:T(8,128)(2,1)} %copy-done.13) | copy-start | bytes 1769476
  824.9 254.3 %reduce-scatter.17.cloned.1.call-start = ((), (), s32[]{:S(2)}) async-start(), calls=%async_computation.13 | async-start | bytes 2654208 | tf_op jit(solution)/shard_map/reduce_scatter | solution.py:280
  830.9 40.5 %copy-start.12 = (bf16[3,512,192]{1,2,0:T(8,128)(2,1)S(1)}, bf16[3,512,192]{1,2,0:T(8,128)(2,1)}, u32[]{:S(2)}) copy-start(bf16[3,512,192]{1,2,0:T(8,128)(2,1)} %copy-done.11) | copy-start | bytes 1769476
  830.9 90.8 %copy-start.10 = (f32[384,768]{1,0:T(8,128)S(1)}, f32[384,768]{1,0:T(8,128)}, u32[]{:S(2)}) copy-start(f32[384,768]{1,0:T(8,128)} %copy-done.9) | copy-start | bytes 3538948
  (28 other events, 107.1 us)
Sparse Core Ops, SparseCore 0:
  9.6 52.6 all-gather.2
  94.7 170.7 all-reduce.5
  291.3 170.9 all-reduce.7
  495.8 48.3 all-gather.4
  558.8 84.0 reduce-scatter.10
  794.1 33.0 reduce-scatter.20
  830.6 40.6 reduce-scatter.18
  874.1 47.5 reduce-scatter.12
  925.0 62.3 all-reduce.9
  991.2 41.6 reduce-scatter.14
  1036.8 42.3 reduce-scatter.16
